TPU v7x, 512 devices: a whole 4x8x8 slice. The times are simulated.
512 devices in a mesh: gx: 32 (over x, z), gy: 2 (over y_hi), gz: 8 (over y_lo, core).
Axes of the slice: x: 4, y: 8 (y_hi: 2, y_lo: 4; y = y_hi * 4 + y_lo), z: 8, core: 2. Of those that a mesh axis runs over, the one named last changes fastest.
Arguments:
- coeffs: bfloat16 [16, 1024, 160], P('gz', ('gx', 'gy')), may hold values from -6 to 6
- translations: bfloat16 [16384, 160, 160], P(('gx', 'gz'), 'gy'), may hold values from -0.25 to 0.25
- tmatrix: bfloat16 [1024, 160, 160], P('gx', 'gy'), may hold values from -0.5 to 0.5
- pair_target: int32 [16384], P('gx'), may hold values from 0 to 31
- pair_source: int32 [16384], P('gx'), may hold values from 0 to 1023, as said below
- pair_count: int32 [32], P('gx'), may hold values from 256 to 512, as said below
Outputs:
- result: bfloat16 [16, 1024, 160], P('gz', ('gx', 'gy'))
Inputs may be any that keep to these rules, and one draw needn't show every extreme that they name: `pair_count`: some gx group has all 512 slots live in every draw. The source sphere of a slot of group g lies in group g - 1, g or g + 1 modulo 32, that is pair_source[p] // 32 is one of these.
All inputs are finite; a program needn't handle non-finite values.
Results may differ from a plain program's by a relative error of at most 0.009.
Values may be sent and summed in bfloat16 or wider, within the bound.
No kernel may reach another device: no remote copies, remote signals or barrier semaphores. Data moves between devices by JAX's collectives and lax.ppermute only.
A program may use at most 64 MiB of HBM per device.

v0:
```python
import jax
import jax.numpy as jnp
from jax import lax
from jax.sharding import PartitionSpec as P


def padded(value, sides, width):
    for axis, dim in sides:
        devices, length = (lax.axis_size(axis), value.shape[dim])
        up = [(i, (i + 1) % devices) for i in range(devices)]
        down = [(j, i) for i, j in up]
        last = lax.slice_in_dim(value, length - width, length, axis=dim)
        leading = lax.slice_in_dim(value, 0, width, axis=dim)
        before = lax.ppermute(last, axis, up)
        after = lax.ppermute(leading, axis, down)
        value = jnp.concatenate([before, value, after], axis=dim)
    return value


def cut_along(value, dim, devices):
    dims = value.shape
    tiles = value.reshape(*dims[:dim], devices, dims[dim] // devices, *dims[dim + 1 :])
    return jnp.moveaxis(tiles, dim, 0)


def sum_at_owner(value, axis, dim):
    tiles = cut_along(value, dim, lax.axis_size(axis))
    arrived = lax.all_to_all(tiles, axis, split_axis=0, concat_axis=0, tiled=True)
    return arrived.sum(axis=0)


def per_device(coeffs, translations, tmatrix, pair_target, pair_source, pair_count):
    spheres_group = tmatrix.shape[0]
    slots_group = pair_target.shape[0]
    slots_device = translations.shape[0]
    groups_all = lax.axis_size("gx")
    own_group = lax.all_gather(coeffs, "gy", axis=1, tiled=True)
    window = padded(own_group, (("gx", 1),), spheres_group)
    here = lax.axis_index("gx")
    source_group = pair_source // spheres_group
    relative = (source_group - here + 1 + groups_all) % groups_all
    local_index = relative * spheres_group + pair_source % spheres_group
    picked = jnp.take(window, local_index, axis=1)
    living = jnp.arange(slots_group, dtype=jnp.int32) < pair_count[0]
    spheres_here = jnp.arange(spheres_group, dtype=jnp.int32)
    select = ((pair_target[None, :] == spheres_here[:, None]) & living[None, :]).astype(jnp.float32)
    gathered_rhs = lax.all_to_all(picked, "gz", split_axis=1, concat_axis=0, tiled=True)
    contrib = jnp.einsum(
        "pkl,rpl->rpk", translations, gathered_rhs, preferred_element_type=jnp.float32
    )
    own_select = lax.dynamic_slice_in_dim(
        select, lax.axis_index("gz") * slots_device, slots_device, 1
    )
    partial_field = jnp.einsum("sp,rpk->rsk", own_select, contrib)
    near_field = sum_at_owner(partial_field, "gz", 0).astype(jnp.bfloat16)
    scattered = jnp.einsum("rsc,sci->rsi", near_field, tmatrix, preferred_element_type=jnp.float32)
    kept_rows = sum_at_owner(scattered, "gy", 1)
    return (coeffs.astype(jnp.float32) - kept_rows).astype(jnp.bfloat16)


def solution(mesh):
    placed = (
        P("gz", ("gx", "gy"), None),
        P(("gx", "gz"), "gy", None),
        P("gx", "gy", None),
        P("gx"),
        P("gx"),
        P("gx"),
    )
    return jax.shard_map(
        per_device,
        mesh=mesh,
        in_specs=placed,
        out_specs=P("gz", ("gx", "gy"), None),
        check_vma=False,
    )
```

profile of v0, /device:TPU:1, one launch (start us, length us, event | category | flops | bytes accessed | tf_op | source)
XLA Modules:
  0.0 79.3 jit_solution(16993245647487317368)
XLA Ops:
  0.0 0.0 copy-start
  0.0 0.9 %copy.16 = bf16[2,16,160]{2,0,1:T(2,128)(2,1)S(1)} copy(bf16[2,16,160]{2,1,0:T(8,128)(2,1)} %param.6) | data formatting | bytes 20480 | tf_op args[0]
  0.9 8.1 %all_gather.3 = bf16[2,32,160]{2,0,1:T(2,128)(2,1)S(1)} all-gather(bf16[2,16,160]{2,0,1:T(2,128)(2,1)S(1)} %copy.16), channel_id=1, replica_groups=mesh['gx'=32,'gy'=2,'gz'=8] {'gy'}, dimensions={1}, use_global_device_ids=true | all-gather | bytes 30720 | tf_op jit(solution)/shard_map/all_gather | solution.py:37
  9.0 4.0 %collective-permute-start = (bf16[2,32,160]{2,0,1:T(2,128)(2,1)S(1)}, bf16[2,32,160]{2,0,1:T(2,128)(2,1)S(1)}, u32[]{:S(2)}, u32[]{:S(2)}) collective-permute-start(bf16[2,32,160]{2,0,1:T(2,128)(2,1)S(1)} %all_gather.3), channel_id=1, source_target_pairs={{0,16},{16,32},{32,48},{48,64},{64,80},{80,96},{96,112},{112,128},... | collective-permute-start | bytes 61448 | tf_op jit(solution)/shard_map/ppermute | solution.py:14
  13.0 10.8 %collective-permute-start.1 = (bf16[2,32,160]{2,0,1:T(2,128)(2,1)S(1)}, bf16[2,32,160]{2,0,1:T(2,128)(2,1)S(1)}, u32[]{:S(2)}, u32[]{:S(2)}) collective-permute-start(bf16[2,32,160]{2,0,1:T(2,128)(2,1)S(1)} %all_gather.3), channel_id=1, source_target_pairs={{16,0},{32,16},{48,32},{64,48},{80,64},{96,80},{112,96},{128,112},... | collective-permute-start | bytes 61448 | tf_op jit(solution)/shard_map/ppermute | solution.py:15
  23.8 0.7 compare_and_fusion
  24.5 0.0 collective-permute-done
  24.6 0.3 collective-permute-done.1
  24.8 0.2 pad_maximum_fusion
  25.0 2.6 %gather_fusion = bf16[512,2,160]{2,1,0:T(2,128)(2,1)S(1)} fusion(bf16[2,96,160]{2,0,1:T(2,128)(2,1)S(1)} %pad_maximum_fusion, s32[1024]{0:T(1024)S(1)} %pad_clamp_fusion), kind=kCustom, calls=%fused_computation | custom fusion | bytes 657408 | tf_op jit(solution)/shard_map/jit(_take)/gather | solution.py:43
  27.6 2.5 %fusion.3 = bf16[2,512,160]{2,0,1:T(2,128)(2,1)} fusion(bf16[512,2,160]{2,1,0:T(2,128)(2,1)S(1)} %gather_fusion, pred[512]{0:T(512)(128)(4,1)S(1)} %get-tuple-element.5), kind=kLoop, calls=%fused_computation.6 | loop fusion | flops 163840 | bytes 655872 | tf_op jit(solution)/shard_map/jit(_take)/select_n | solution.py:43
  30.1 7.4 %all-to-all-start = ((bf16[2,512,160]{2,0,1:T(2,128)(2,1)}), bf16[2,512,160]{2,0,1:T(2,128)(2,1)S(1)}, u32[]{:S(2)}, u32[]{:S(2)}) async-start(bf16[2,512,160]{2,0,1:T(2,128)(2,1)} %fusion.3), calls=%async_computation | async-start | bytes 1048576 | tf_op jit(solution)/shard_map/all_to_all | solution.py:47
  38.1 0.1 dynamic-slice.1
  38.2 0.8 dynamic-slice
  38.9 12.9 %all-to-all-done = bf16[2,512,160]{2,0,1:T(2,128)(2,1)S(1)} async-done(((bf16[2,512,160]{2,0,1:T(2,128)(2,1)}), bf16[2,512,160]{2,0,1:T(2,128)(2,1)S(1)}, u32[]{:S(2)}, u32[]{:S(2)}) %all-to-all-start) | async-done | bytes 327712 | tf_op jit(solution)/shard_map/all_to_all | solution.py:47
  51.8 0.1 copy.17
  51.9 0.0 copy-start.1
  51.9 0.8 %convolution_bitcast_fusion = bf16[16,64,80]{2,0,1:T(8,128)(2,1)S(1)} fusion(bf16[64,80,160]{2,1,0:T(8,128)(2,1)S(1)} %copy-done, bf16[16,64,160]{2,1,0:T(8,128)(2,1)S(1)} %bitcast.24), kind=kOutput, calls=%fused_computation.1 | convolution fusion | flops 26214400 | bytes 2129920 | tf_op jit(solution)/shard_map/pkl,rpl->rpk/dot_general | solution.py:48
  52.7 0.2 fusion
  52.9 12.0 %all_to_all.28 = f32[8,2,32,80]{3,2,1,0:T(8,128)S(1)} all-to-all(f32[8,2,32,80]{3,2,1,0:T(8,128)S(1)} %bitcast.25), channel_id=1, replica_groups=mesh['gx'=32,'gy'=2,'gz'=8] {'gz'}, dimensions={0} | all-to-all | bytes 327680 | tf_op jit(solution)/shard_map/all_to_all | solution.py:28
  65.0 1.6 %fusion.5 = f32[32,2,160]{2,1,0:T(2,128)S(1)} fusion(bf16[32,80,160]{2,1,0:T(8,128)(2,1)} %param.8, bf16[2,32,80]{2,1,0:T(8,128)(2,1)S(1)} %reduce_sum.18), kind=kOutput, calls=%fused_computation.11 | convolution fusion | flops 1638400 | bytes 870400 | tf_op jit(solution)/shard_map/rsc,sci->rsi/dot_general | solution.py:56
  66.6 12.0 %all_to_all.29 = f32[2,2,16,160]{3,1,2,0:T(2,128)S(1)} all-to-all(f32[2,2,16,160]{3,1,2,0:T(2,128)S(1)} %bitcast.26), channel_id=1, replica_groups=mesh['gx'=32,'gy'=2,'gz'=8] {'gy'}, dimensions={0} | all-to-all | bytes 81920 | tf_op jit(solution)/shard_map/all_to_all | solution.py:28
  78.7 0.0 copy-done.1
  78.7 0.6 fusion.4
  (5 shorter events, 0.1 us)
Async XLA Ops:
  0.0 51.9 %copy-start = (bf16[64,80,160]{2,1,0:T(8,128)(2,1)S(1)}, bf16[64,80,160]{2,1,0:T(8,128)(2,1)}, u32[]{:S(2)}) copy-start(bf16[64,80,160]{2,1,0:T(8,128)(2,1)} %param.7) | copy-start | bytes 4915204
  9.0 15.5 %collective-permute-start = (bf16[2,32,160]{2,0,1:T(2,128)(2,1)S(1)}, bf16[2,32,160]{2,0,1:T(2,128)(2,1)S(1)}, u32[]{:S(2)}, u32[]{:S(2)}) collective-permute-start(bf16[2,32,160]{2,0,1:T(2,128)(2,1)S(1)} %all_gather.3), channel_id=1, source_target_pairs={{0,16},{16,32},{32,48},{48,64},{64,80},{80,96},{96,112},{112,128},... | collective-permute-start | bytes 61448 | tf_op jit(solution)/shard_map/ppermute | solution.py:14
  13.0 11.8 %collective-permute-start.1 = (bf16[2,32,160]{2,0,1:T(2,128)(2,1)S(1)}, bf16[2,32,160]{2,0,1:T(2,128)(2,1)S(1)}, u32[]{:S(2)}, u32[]{:S(2)}) collective-permute-start(bf16[2,32,160]{2,0,1:T(2,128)(2,1)S(1)} %all_gather.3), channel_id=1, source_target_pairs={{16,0},{32,16},{48,32},{64,48},{80,64},{96,80},{112,96},{128,112},... | collective-permute-start | bytes 61448 | tf_op jit(solution)/shard_map/ppermute | solution.py:15
  30.1 21.8 %all-to-all-start = ((bf16[2,512,160]{2,0,1:T(2,128)(2,1)}), bf16[2,512,160]{2,0,1:T(2,128)(2,1)S(1)}, u32[]{:S(2)}, u32[]{:S(2)}) async-start(bf16[2,512,160]{2,0,1:T(2,128)(2,1)} %fusion.3), calls=%async_computation | async-start | bytes 1048576 | tf_op jit(solution)/shard_map/all_to_all | solution.py:47
  51.9 26.8 %copy-start.1 = (bf16[2,16,160]{2,1,0:T(8,128)(2,1)S(1)}, bf16[2,16,160]{2,1,0:T(8,128)(2,1)}, u32[]{:S(2)}) copy-start(bf16[2,16,160]{2,1,0:T(8,128)(2,1)} %param.6) | copy-start | bytes 30724
where the time goes:
time: 79.7 us; the launch traced here: 79.3 us
  blocking collectives  32.2 us (40%)
  starting transfers between devices  22.2 us (28%)
  waiting for transfers between devices  13.1 us (16%)
  local copies, waits for them, and re-layouts  4.37 us (5%)
  other arithmetic  4.05 us (5%)
  matrix products  2.6 us (3%)
    all_to_all x2, blocking collectives, sum_at_owner(): lax.all_to_all(tiles, axis, split_axis=0, concat_axis=0, tiled=True)  24.1 us
    all_to_all x1, waiting for transfers between devices, per_device(): lax.all_to_all(picked, 'gz', split_axis=1, concat_axis=0, tiled=True)  12.9 us
    ppermute x1, starting transfers between devices, padded(): after = lax.ppermute(leading, axis, down)  10.8 us
    all_gather x1, blocking collectives, per_device(): own_group = lax.all_gather(coeffs, 'gy', axis=1, tiled=True)  8.15 us
    all_to_all x1, starting transfers between devices, per_device(): lax.all_to_all(picked, 'gz', split_axis=1, concat_axis=0, tiled=True)  7.39 us
    ppermute x1, starting transfers between devices, padded(): before = lax.ppermute(last, axis, up)  3.99 us
    gather x1, local copies, waits for them, and re-layouts, per_device(): picked = jnp.take(window, local_index, axis=1)  2.57 us
    select_n x1, other arithmetic, per_device(): picked = jnp.take(window, local_index, axis=1)  2.5 us
  transfers between devices with their start and end apart: 3, of which 2 were waited for; matrix products, arithmetic and copies ran while one was open for 2% of the time, Pallas kernels for 0%

commit v1 on v0

v1 whole, which is shorter than its diff:
```python
import functools

import jax
import jax.numpy as jnp
from jax import lax
from jax.experimental import pallas as pl
from jax.experimental.pallas import tpu as pltpu
from jax.sharding import PartitionSpec as P

LANES = 128
COLUMN = ("gy", "gz")


def pack_rows(full, rest):
    rows = full.shape[0]
    quarter = rows // 4
    lane = lax.broadcasted_iota(jnp.int32, (quarter, LANES), 1)
    packed = rest[:quarter]
    for q in range(1, 4):
        part = pltpu.roll(rest[q * quarter : (q + 1) * quarter], 32 * q, 1)
        packed = jnp.where(lane < 32 * q, packed, part)
    return jnp.concatenate([full, packed], axis=0)


def unpack_rest(packed):
    parts = [packed] + [pltpu.roll(packed, LANES - 32 * q, 1) for q in range(1, 4)]
    return jnp.concatenate(parts, axis=0)


def widen(value):
    rows = value.shape[0]
    return jnp.concatenate([value, jnp.zeros((rows, LANES - value.shape[1]), value.dtype)], axis=1)


def pack_kernel(x_ref, out_ref):
    rhs, spheres, length = x_ref.shape
    x = x_ref[...].astype(jnp.float32).reshape(rhs * spheres, length)
    packed = pack_rows(x[:, :LANES], widen(x[:, LANES:])).astype(jnp.bfloat16)
    for d in range(out_ref.shape[0]):
        out_ref[d] = packed


def field_kernel(
    target_ref, source_ref, count_ref, own_ref, a_ref, b_ref, trans_ref, tmat_ref, out_ref,
    full_ref, rest_ref, near_ref, sfull_ref, srest_ref,
):
    here = lax.axis_index("gx")
    groups = lax.axis_size("gx")
    base = lax.axis_index("gz") * trans_ref.shape[0]
    spheres = tmat_ref.shape[0]
    half = spheres // 2
    members = own_ref.shape[0]
    rows = own_ref.shape[1] * 4 // 5
    length = trans_ref.shape[2]
    for b, ref in enumerate((own_ref, a_ref, b_ref)):
        for d in range(members):
            piece = ref[d].astype(jnp.float32)
            at = (b * members + d) * rows
            full_ref[at : at + rows, :] = piece[:rows]
            rest_ref[at : at + rows, :] = unpack_rest(piece[rows:])
    near_ref[...] = jnp.zeros_like(near_ref)
    even = lax.rem(here, 2) == 0
    for p in range(trans_ref.shape[0]):
        source = source_ref[base + p]
        group = lax.div(source, spheres)
        sphere = lax.rem(source, spheres)
        relative = lax.rem(group - here + 1 + groups, groups)
        block = jnp.where(relative == 1, 0, jnp.where((relative == 2) == even, 1, 2))
        start = (block * members + lax.div(sphere, half) * (members // 2)) * rows + lax.rem(sphere, half)
        picked = []
        for r in range(2):
            at = pl.ds(start + r * half, members // 2, stride=rows)
            picked.append(
                jnp.concatenate([full_ref[at, :], rest_ref[at, :][:, : length - LANES]], axis=1)
            )
        x = jnp.concatenate(picked, axis=0).astype(jnp.bfloat16)
        contrib = lax.dot_general(
            x, trans_ref[p], (((1,), (1,)), ((), ())), preferred_element_type=jnp.float32
        )
        slot = jnp.where(base + p < count_ref[0], target_ref[base + p], spheres)
        near_ref[slot] = near_ref[slot] + contrib
    for s in range(spheres):
        near = near_ref[s].astype(jnp.bfloat16)
        scattered = jnp.dot(near, tmat_ref[s], preferred_element_type=jnp.float32)
        start = (s // half) * (members // 2) * rows + s % half
        for r in range(2):
            at = pl.ds(start + r * half, members // 2, stride=rows)
            part = scattered[r * (members // 2) : (r + 1) * (members // 2)]
            sfull_ref[at, :] = part[:, :LANES]
            srest_ref[at, :] = widen(part[:, LANES:])
    for d in range(members):
        at = slice(d * rows, (d + 1) * rows)
        out_ref[d] = pack_rows(sfull_ref[at, :], srest_ref[at, :]).astype(jnp.bfloat16)


def final_kernel(x_ref, parts_ref, out_ref):
    rhs, spheres, length = x_ref.shape
    rows = rhs * spheres
    total = parts_ref[0].astype(jnp.float32)
    for d in range(1, parts_ref.shape[0]):
        total = total + parts_ref[d].astype(jnp.float32)
    rest = unpack_rest(total[rows:])[:, : length - LANES]
    scattered = jnp.concatenate([total[:rows], rest], axis=1)
    x = x_ref[...].astype(jnp.float32).reshape(rows, length)
    out_ref[...] = (x - scattered).astype(jnp.bfloat16).reshape(rhs, spheres, length)


def vmem(count):
    return [pl.BlockSpec(memory_space=pltpu.VMEM)] * count


def per_device(coeffs, translations, tmatrix, pair_target, pair_source, pair_count):
    groups = lax.axis_size("gx")
    members = lax.axis_size("gy") * lax.axis_size("gz")
    rhs, spheres, length = coeffs.shape
    rows = rhs * spheres
    packed = rows * length // LANES
    piece = jax.ShapeDtypeStruct((members, packed, LANES), jnp.bfloat16)
    shards = pl.pallas_call(
        pack_kernel, out_shape=piece, in_specs=vmem(1), out_specs=vmem(1)[0], name="pack"
    )(coeffs)
    own = lax.all_to_all(shards, COLUMN, split_axis=0, concat_axis=0, tiled=True)
    pairs_a = [(g, g ^ 1) for g in range(groups)]
    pairs_b = [(g, (g + 1 if g % 2 else g - 1) % groups) for g in range(groups)]
    side_a = lax.ppermute(own, "gx", pairs_a)
    side_b = lax.ppermute(own, "gx", pairs_b)
    smem = pl.BlockSpec(memory_space=pltpu.SMEM)
    window = 3 * members * rows
    parts = pl.pallas_call(
        field_kernel,
        out_shape=piece,
        in_specs=[smem, smem, smem] + vmem(5),
        out_specs=vmem(1)[0],
        scratch_shapes=[
            pltpu.VMEM((window, LANES), jnp.float32),
            pltpu.VMEM((window, LANES), jnp.float32),
            pltpu.VMEM((tmatrix.shape[0] + 1, members, translations.shape[1]), jnp.float32),
            pltpu.VMEM((members * rows, LANES), jnp.float32),
            pltpu.VMEM((members * rows, LANES), jnp.float32),
        ],
        name="field",
    )(pair_target, pair_source, pair_count, own, side_a, side_b, translations, tmatrix)
    arrived = lax.all_to_all(parts, COLUMN, split_axis=0, concat_axis=0, tiled=True)
    return pl.pallas_call(
        final_kernel,
        out_shape=jax.ShapeDtypeStruct(coeffs.shape, coeffs.dtype),
        in_specs=vmem(2),
        out_specs=vmem(1)[0],
        name="final",
    )(coeffs, arrived)


def solution(mesh):
    placed = (
        P("gz", ("gx", "gy"), None),
        P(("gx", "gz"), "gy", None),
        P("gx", "gy", None),
        P("gx"),
        P("gx"),
        P("gx"),
    )
    return jax.shard_map(
        per_device,
        mesh=mesh,
        in_specs=placed,
        out_specs=P("gz", ("gx", "gy"), None),
        check_vma=False,
    )
```

time: 79.7 us -> 62.3 us (0.78)
  starting transfers between devices: 22.2 us -> 13.1 us
  waiting for transfers between devices: 13.1 us -> 5.03 us
  Pallas kernels: 0 us -> 8.01 us
  other arithmetic: 4.05 us -> 0 us
  local copies, waits for them, and re-layouts: 4.37 us -> 0.67 us
  matrix products: 2.6 us -> 0 us
  blocking collectives: 32.2 us -> 34.3 us
    all_to_all x1 -> x0, waiting for transfers between devices: 12.9 us -> none  [per_device(): lax.all_to_all(picked, 'gz', split_axis=1, concat_axis=0, tiled=True)]
    all_to_all x2, blocking collectives: 24.1 us -> 34.3 us  [the longest x1 19.7 us: per_device(): lax.all_to_all(shards, COLUMN, split_axis=0, concat_axis=0, tiled=True)]
    all_gather x1 -> x0, blocking collectives: 8.15 us -> none  [per_device(): own_group = lax.all_gather(coeffs, 'gy', axis=1, tiled=True)]
    pallas_call x0 -> x3, Pallas kernels: none -> 8.01 us  [the longest x1 4.93 us: per_device(): pl.pallas_call(field_kernel, out_shape=piece, in_specs=[smem, smem, smem]...]
    all_to_all x1 -> x0, starting transfers between devices: 7.39 us -> none  [per_device(): lax.all_to_all(picked, 'gz', split_axis=1, concat_axis=0, tiled=True)]
    ppermute x2, waiting for transfers between devices: 0.27 us -> 5.03 us  [the longest x1 2.96 us: per_device(): side_a = lax.ppermute(own, 'gx', pairs_a)]
    dot_general x3 -> x0, matrix products: 2.6 us -> none  [the longest x1 1.59 us: per_device(): jnp.einsum('rsc,sci->rsi', near_field, tmatrix, preferred_element_type=jn...]
    gather x1 -> x0, local copies, waits for them, and re-layouts: 2.57 us -> none  [per_device(): picked = jnp.take(window, local_index, axis=1)]
  transfers between devices with their start and end apart: 3 -> 2, of which waited for: 2 -> 2; matrix products, arithmetic and copies ran while one was open for 2% -> 0% of each run, Pallas kernels for 0% -> 0%
where the time goes in v1:
time: 62.3 us; the launch traced here: 61.8 us
  blocking collectives  34.3 us (55%)
  starting transfers between devices  13.1 us (21%)
  Pallas kernels  8.01 us (13%)
  waiting for transfers between devices  5.03 us (8%)
  local copies, waits for them, and re-layouts  0.67 us (1%)
  between operations  0.67 us (1%)
    all_to_all x1, blocking collectives, per_device(): lax.all_to_all(shards, COLUMN, split_axis=0, concat_axis=0, tiled=True)  19.7 us
    all_to_all x1, blocking collectives, per_device(): lax.all_to_all(parts, COLUMN, split_axis=0, concat_axis=0, tiled=True)  14.5 us
    ppermute x1, starting transfers between devices, per_device(): side_b = lax.ppermute(own, 'gx', pairs_b)  11.2 us
    pallas_call x1, Pallas kernels, per_device(): pl.pallas_call(field_kernel, out_shape=piece, in_specs=[smem, smem, smem]...  4.93 us
    ppermute x1, waiting for transfers between devices, per_device(): side_a = lax.ppermute(own, 'gx', pairs_a)  2.96 us
    ppermute x1, waiting for transfers between devices, per_device(): side_b = lax.ppermute(own, 'gx', pairs_b)  2.06 us
    ppermute x1, starting transfers between devices, per_device(): side_a = lax.ppermute(own, 'gx', pairs_a)  1.92 us
    pallas_call x1, Pallas kernels, per_device(): pl.pallas_call(final_kernel, out_shape=jax.ShapeDtypeStruct(coeffs.shape,...  1.63 us
  transfers between devices with their start and end apart: 2, of which 2 were waited for; matrix products, arithmetic and copies ran while one was open for 0% of the time, Pallas kernels for 0%

profile of v1, /device:TPU:1, one launch (start us, length us, event | category | flops | bytes accessed | tf_op | source)
XLA Modules:
  0.0 61.8 jit_solution(16320921602172925679)
XLA Ops:
  0.0 1.4 %pack.1 = bf16[16,40,128]{2,1,0:T(8,128)(2,1)} custom-call(bf16[2,16,160]{2,1,0:T(8,128)(2,1)} %x_ref.3), custom_call_target="tpu_custom_call" | custom-call | tf_op jit(solution)/shard_map/pack/pallas_call | solution.py:119
  1.5 19.7 %all_to_all.10.own_ref = bf16[16,40,128]{2,1,0:T(8,128)(2,1)S(1)} all-to-all(bf16[16,40,128]{2,1,0:T(8,128)(2,1)} %pack.1), channel_id=1, replica_groups=mesh['gx'=32,'gy'=2,'gz'=8] {'gy','gz'}, dimensions={0} | all-to-all | bytes 327680 | tf_op jit(solution)/shard_map/all_to_all | solution.py:122
  21.2 0.0 copy-start
  21.2 11.2 %collective-permute-start.1 = (bf16[16,40,128]{2,1,0:T(8,128)(2,1)S(1)}, bf16[16,40,128]{2,1,0:T(8,128)(2,1)S(1)}, u32[]{:S(2)}, u32[]{:S(2)}) collective-permute-start(bf16[16,40,128]{2,1,0:T(8,128)(2,1)S(1)} %all_to_all.10.own_ref), channel_id=1, source_target_pairs={{0,496},{16,32},{32,16},{48,64},{64,48},{80,96},{96,80},{112,128},... | collective-permute-start | bytes 491528 | tf_op jit(solution)/shard_map/ppermute | solution.py:126
  32.4 1.9 %collective-permute-start = (bf16[16,40,128]{2,1,0:T(8,128)(2,1)S(1)}, bf16[16,40,128]{2,1,0:T(8,128)(2,1)S(1)}, u32[]{:S(2)}, u32[]{:S(2)}) collective-permute-start(bf16[16,40,128]{2,1,0:T(8,128)(2,1)S(1)} %all_to_all.10.own_ref), channel_id=1, source_target_pairs={{0,16},{16,0},{32,48},{48,32},{64,80},{80,64},{96,112},{112,96},{1... | collective-permute-start | bytes 491528 | tf_op jit(solution)/shard_map/ppermute | solution.py:125
  35.0 2.1 %collective-permute-done.1.b_ref = bf16[16,40,128]{2,1,0:T(8,128)(2,1)S(1)} collective-permute-done((bf16[16,40,128]{2,1,0:T(8,128)(2,1)S(1)}, bf16[16,40,128]{2,1,0:T(8,128)(2,1)S(1)}, u32[]{:S(2)}, u32[]{:S(2)}) %collective-permute-start.1) | collective-permute-done | bytes 163872 | tf_op jit(solution)/shard_map/ppermute | solution.py:126
  37.1 0.0 copy-start.1
  37.1 3.0 %collective-permute-done.a_ref = bf16[16,40,128]{2,1,0:T(8,128)(2,1)S(1)} collective-permute-done((bf16[16,40,128]{2,1,0:T(8,128)(2,1)S(1)}, bf16[16,40,128]{2,1,0:T(8,128)(2,1)S(1)}, u32[]{:S(2)}, u32[]{:S(2)}) %collective-permute-start) | collective-permute-done | bytes 163872 | tf_op jit(solution)/shard_map/ppermute | solution.py:125
  40.0 0.0 copy-done
  40.0 0.0 copy-done.1
  40.0 0.0 copy-start.2
  40.0 0.7 %copy-done.2 = bf16[16,40,128]{2,1,0:T(8,128)(2,1)} copy-done((bf16[16,40,128]{2,1,0:T(8,128)(2,1)}, bf16[16,40,128]{2,1,0:T(8,128)(2,1)S(1)}, u32[]{:S(2)}) %copy-start.2) | copy-done | bytes 163864
  40.7 4.9 %field.1 = bf16[16,40,128]{2,1,0:T(8,128)(2,1)} custom-call(s32[512]{0:T(512)} %target_ref.1, s32[512]{0:T(512)} %source_ref.1, s32[1]{0:T(128)S(6)} %copy.7.count_ref, bf16[16,40,128]{2,1,0:T(8,128)(2,1)} %copy-done, bf16[16,40,128]{2,1,0:T(8,128)(2,1)} %copy-done.2, bf16[16,40,128]{2,1,0:T(8,128)(2,1)} %copy-done.1, bf16[64,80,160]{2,1,0:T(8,128)(2,1)} %trans_ref.1, ...), custom_call_target="tpu_custom_call" | custom-call | tf_op jit(solution)/shard_map/field/pallas_call | solution.py:129
  45.6 14.5 %all_to_all.11.parts_ref = bf16[16,40,128]{2,1,0:T(8,128)(2,1)} all-to-all(bf16[16,40,128]{2,1,0:T(8,128)(2,1)} %field.1), channel_id=1, replica_groups=mesh['gx'=32,'gy'=2,'gz'=8] {'gy','gz'}, dimensions={0} | all-to-all | bytes 327680 | tf_op jit(solution)/shard_map/all_to_all | solution.py:143
  60.2 1.6 %final.1 = bf16[2,16,160]{2,1,0:T(8,128)(2,1)} custom-call(bf16[2,16,160]{2,1,0:T(8,128)(2,1)} %x_ref.3, bf16[16,40,128]{2,1,0:T(8,128)(2,1)} %all_to_all.11.parts_ref), custom_call_target="tpu_custom_call" | custom-call | tf_op jit(solution)/shard_map/final/pallas_call | solution.py:144
Async XLA Ops:
  21.2 18.8 %copy-start = (bf16[16,40,128]{2,1,0:T(8,128)(2,1)}, bf16[16,40,128]{2,1,0:T(8,128)(2,1)S(1)}, u32[]{:S(2)}) copy-start(bf16[16,40,128]{2,1,0:T(8,128)(2,1)S(1)} %all_to_all.10.own_ref) | copy-start | bytes 491524
  21.2 15.9 %collective-permute-start.1 = (bf16[16,40,128]{2,1,0:T(8,128)(2,1)S(1)}, bf16[16,40,128]{2,1,0:T(8,128)(2,1)S(1)}, u32[]{:S(2)}, u32[]{:S(2)}) collective-permute-start(bf16[16,40,128]{2,1,0:T(8,128)(2,1)S(1)} %all_to_all.10.own_ref), channel_id=1, source_target_pairs={{0,496},{16,32},{32,16},{48,64},{64,48},{80,96},{96,80},{112,128},... | collective-permute-start | bytes 491528 | tf_op jit(solution)/shard_map/ppermute | solution.py:126
  32.4 7.6 %collective-permute-start = (bf16[16,40,128]{2,1,0:T(8,128)(2,1)S(1)}, bf16[16,40,128]{2,1,0:T(8,128)(2,1)S(1)}, u32[]{:S(2)}, u32[]{:S(2)}) collective-permute-start(bf16[16,40,128]{2,1,0:T(8,128)(2,1)S(1)} %all_to_all.10.own_ref), channel_id=1, source_target_pairs={{0,16},{16,0},{32,48},{48,32},{64,80},{80,64},{96,112},{112,96},{1... | collective-permute-start | bytes 491528 | tf_op jit(solution)/shard_map/ppermute | solution.py:125
  37.1 3.0 %copy-start.1 = (bf16[16,40,128]{2,1,0:T(8,128)(2,1)}, bf16[16,40,128]{2,1,0:T(8,128)(2,1)S(1)}, u32[]{:S(2)}) copy-start(bf16[16,40,128]{2,1,0:T(8,128)(2,1)S(1)} %collective-permute-done.1.b_ref) | copy-start | bytes 491524
  40.0 0.7 %copy-start.2 = (bf16[16,40,128]{2,1,0:T(8,128)(2,1)}, bf16[16,40,128]{2,1,0:T(8,128)(2,1)S(1)}, u32[]{:S(2)}) copy-start(bf16[16,40,128]{2,1,0:T(8,128)(2,1)S(1)} %collective-permute-done.a_ref) | copy-start | bytes 491524

commit v2 on v1

v2 whole, which is shorter than its diff:
```python
import jax
import jax.numpy as jnp
from jax import lax
from jax.experimental import pallas as pl
from jax.experimental.pallas import tpu as pltpu
from jax.sharding import PartitionSpec as P


LANES = 128
COLUMN = ("gy", "gz")
CHUNKS = 4
VMEM = pl.BlockSpec(memory_space=pltpu.VMEM)
SMEM = pl.BlockSpec(memory_space=pltpu.SMEM)
HBM = pl.BlockSpec(memory_space=pltpu.HBM)


def pack_rows(full, rest):
    quarter = full.shape[0] // 4
    lane = lax.broadcasted_iota(jnp.int32, (quarter, LANES), 1)
    packed = rest[:quarter]
    for q in range(1, 4):
        part = pltpu.roll(rest[q * quarter : (q + 1) * quarter], 32 * q, 1)
        packed = jnp.where(lane < 32 * q, packed, part)
    return jnp.concatenate([full, packed], axis=0)


def unpack_rest(packed):
    parts = [packed] + [pltpu.roll(packed, LANES - 32 * q, 1) for q in range(1, 4)]
    return jnp.concatenate(parts, axis=0)


def widen(value):
    rows = value.shape[0]
    return jnp.concatenate([value, jnp.zeros((rows, LANES - value.shape[1]), value.dtype)], axis=1)


def pack_kernel(x_ref, out_ref):
    rhs, spheres, length = x_ref.shape
    x = x_ref[...].astype(jnp.float32).reshape(rhs * spheres, length)
    packed = pack_rows(x[:, :LANES], widen(x[:, LANES:])).astype(jnp.bfloat16)
    for d in range(out_ref.shape[0]):
        out_ref[d] = packed


def field_kernel(
    start_ref, slot_ref, left_ref, own_ref, right_ref, trans_hbm, tmat_hbm, out_ref,
    trans_ref, tmat_ref, full_ref, rest_ref, near_ref, sfull_ref, srest_ref, sems,
):
    slots = trans_ref.shape[0]
    spheres = tmat_ref.shape[0]
    part = slots // CHUNKS
    copies = [
        pltpu.make_async_copy(
            trans_hbm.at[pl.ds(c * part, part)], trans_ref.at[pl.ds(c * part, part)], sems.at[c]
        )
        for c in range(CHUNKS)
    ]
    copies.append(pltpu.make_async_copy(tmat_hbm, tmat_ref, sems.at[CHUNKS]))
    for copy in copies:
        copy.start()
    half = spheres // 2
    length = trans_ref.shape[2]
    members = near_ref.shape[1]
    rows = full_ref.shape[0] // (3 * members)

    def place(piece, at):
        piece = piece.astype(jnp.float32)
        full_ref[pl.ds(at, rows), :] = piece[:rows]
        rest_ref[pl.ds(at, rows), :] = unpack_rest(piece[rows:])

    for b, ref in enumerate((left_ref, own_ref, right_ref)):
        for d in range(members):
            place(ref[d], (b * members + d) * rows)
    near_ref[...] = jnp.zeros_like(near_ref)
    for p in range(slots):
        if p % part == 0:
            copies[p // part].wait()
        start = start_ref[p]
        picked = []
        for r in range(2):
            at = pl.ds(start + r * half, members // 2, stride=rows)
            picked.append(
                jnp.concatenate([full_ref[at, :], rest_ref[at, :][:, : length - LANES]], axis=1)
            )
        x = jnp.concatenate(picked, axis=0).astype(jnp.bfloat16)
        contrib = lax.dot_general(
            x, trans_ref[p], (((1,), (1,)), ((), ())), preferred_element_type=jnp.float32
        )
        slot = slot_ref[p]
        near_ref[slot] = near_ref[slot] + contrib
    copies[CHUNKS].wait()
    for s in range(spheres):
        near = near_ref[s].astype(jnp.bfloat16)
        scattered = jnp.dot(near, tmat_ref[s], preferred_element_type=jnp.float32)
        start = (s // half) * (members // 2) * rows + s % half
        for r in range(2):
            at = pl.ds(start + r * half, members // 2, stride=rows)
            value = scattered[r * (members // 2) : (r + 1) * (members // 2)]
            sfull_ref[at, :] = value[:, :LANES]
            srest_ref[at, :] = widen(value[:, LANES:])
    for d in range(members):
        at = slice(d * rows, (d + 1) * rows)
        out_ref[d] = pack_rows(sfull_ref[at, :], srest_ref[at, :]).astype(jnp.bfloat16)


def final_kernel(x_ref, parts_ref, out_ref):
    rhs, spheres, length = x_ref.shape
    rows = rhs * spheres
    total = parts_ref[0].astype(jnp.float32)
    for d in range(1, parts_ref.shape[0]):
        total = total + parts_ref[d].astype(jnp.float32)
    rest = unpack_rest(total[rows:])[:, : length - LANES]
    scattered = jnp.concatenate([total[:rows], rest], axis=1)
    x = x_ref[...].astype(jnp.float32).reshape(rows, length)
    out_ref[...] = (x - scattered).astype(jnp.bfloat16).reshape(rhs, spheres, length)


def limit(mebibytes):
    return pltpu.CompilerParams(vmem_limit_bytes=mebibytes * 2**20)


def bf16(*shape):
    return jax.ShapeDtypeStruct(shape, jnp.bfloat16)


def per_device(coeffs, translations, tmatrix, pair_target, pair_source, pair_count):
    groups = lax.axis_size("gx")
    members = lax.axis_size("gy") * lax.axis_size("gz")
    rhs, spheres, length = coeffs.shape
    rows = rhs * spheres
    packed = rows * length // LANES
    up = [(g, (g + 1) % groups) for g in range(groups)]
    down = [(g, (g - 1) % groups) for g in range(groups)]
    shards = pl.pallas_call(
        pack_kernel, out_shape=bf16(members, packed, LANES), in_specs=[VMEM], out_specs=VMEM,
        compiler_params=limit(2), name="pack",
    )(coeffs)
    own = lax.all_to_all(shards, COLUMN, split_axis=0, concat_axis=0, tiled=True)
    left = lax.ppermute(own, "gx", up)
    right = lax.ppermute(own, "gx", down)
    window = (left, own, right)
    rows_window = 3 * members * rows
    slots = translations.shape[0]
    group_spheres = tmatrix.shape[0]
    base = lax.axis_index("gz") * slots
    source = lax.dynamic_slice_in_dim(pair_source, base, slots)
    target = lax.dynamic_slice_in_dim(pair_target, base, slots)
    relative = (source // group_spheres - lax.axis_index("gx") + 1 + groups) % groups
    sphere = source % group_spheres
    holder = (relative * 2 + sphere // spheres) * (members // 2)
    start = holder * rows + sphere % spheres
    living = base + jnp.arange(slots, dtype=jnp.int32) < pair_count[0]
    slot = jnp.where(living, target, group_spheres)
    parts = pl.pallas_call(
        field_kernel,
        out_shape=bf16(members, packed, LANES),
        in_specs=[SMEM] * 2 + [VMEM] * len(window) + [HBM] * 2,
        out_specs=VMEM,
        scratch_shapes=[
            pltpu.VMEM(translations.shape, jnp.bfloat16),
            pltpu.VMEM(tmatrix.shape, jnp.bfloat16),
            pltpu.VMEM((rows_window, LANES), jnp.float32),
            pltpu.VMEM((rows_window, LANES), jnp.float32),
            pltpu.VMEM((tmatrix.shape[0] + 1, members, translations.shape[1]), jnp.float32),
            pltpu.VMEM((members * rows, LANES), jnp.float32),
            pltpu.VMEM((members * rows, LANES), jnp.float32),
            pltpu.SemaphoreType.DMA((CHUNKS + 1,)),
        ],
        compiler_params=limit(53),
        name="field",
    )(start, slot, *window, translations, tmatrix)
    arrived = lax.all_to_all(parts, COLUMN, split_axis=0, concat_axis=0, tiled=True)
    return pl.pallas_call(
        final_kernel, out_shape=bf16(*coeffs.shape), in_specs=[VMEM] * 2, out_specs=VMEM,
        compiler_params=limit(2), name="final",
    )(coeffs, arrived)


def solution(mesh):
    placed = (
        P("gz", ("gx", "gy"), None),
        P(("gx", "gz"), "gy", None),
        P("gx", "gy", None),
        P("gx"),
        P("gx"),
        P("gx"),
    )
    return jax.shard_map(
        per_device,
        mesh=mesh,
        in_specs=placed,
        out_specs=P("gz", ("gx", "gy"), None),
        check_vma=False,
    )
```

time: 62.3 us -> 60.1 us (0.965)
  Pallas kernels: 8.01 us -> 4.24 us
  waiting for transfers between devices: 5.03 us -> 7.54 us
  blocking collectives: 34.3 us -> 31.9 us
  other arithmetic: 0 us -> 0.8 us
  starting transfers between devices: 13.1 us -> 13.8 us
    pallas_call x3, Pallas kernels: 8.01 us -> 4.24 us  [the longest x1 3.46 us: per_device(): pl.pallas_call(field_kernel, out_shape=bf16(members, packed, LANES), in_s...]
    ppermute x2, waiting for transfers between devices: 5.03 us -> 7.54 us  [the longest x1 7.16 us: per_device(): left = lax.ppermute(own, 'gx', up)]
    all_to_all x1, blocking collectives: 14.5 us -> 12.9 us  [per_device(): lax.all_to_all(parts, COLUMN, split_axis=0, concat_axis=0, tiled=True)]
    select_n x0 -> x1, other arithmetic: none -> 0.8 us  [per_device(): slot = jnp.where(living, target, group_spheres)]
    all_to_all x1, blocking collectives: 19.7 us -> 19 us  [per_device(): lax.all_to_all(shards, COLUMN, split_axis=0, concat_axis=0, tiled=True)]
    ppermute x2, starting transfers between devices: 13.1 us -> 13.8 us  [the longest x1 11.9 us: per_device(): right = lax.ppermute(own, 'gx', down)]
  transfers between devices with their start and end apart: 2 -> 2, of which waited for: 2 -> 2; matrix products, arithmetic and copies ran while one was open for 0% -> 1% of each run, Pallas kernels for 0% -> 0%
where the time goes in v2:
time: 60.1 us; the launch traced here: 59.7 us
  blocking collectives  31.9 us (53%)
  starting transfers between devices  13.8 us (23%)
  waiting for transfers between devices  7.54 us (13%)
  Pallas kernels  4.24 us (7%)
  other arithmetic  0.8 us (1%)
  local copies, waits for them, and re-layouts  0.72 us (1%)
  between operations  0.68 us (1%)
    all_to_all x1, blocking collectives, per_device(): lax.all_to_all(shards, COLUMN, split_axis=0, concat_axis=0, tiled=True)  19 us
    all_to_all x1, blocking collectives, per_device(): lax.all_to_all(parts, COLUMN, split_axis=0, concat_axis=0, tiled=True)  12.9 us
    ppermute x1, starting transfers between devices, per_device(): right = lax.ppermute(own, 'gx', down)  11.9 us
    ppermute x1, waiting for transfers between devices, per_device(): left = lax.ppermute(own, 'gx', up)  7.16 us
    pallas_call x1, Pallas kernels, per_device(): pl.pallas_call(field_kernel, out_shape=bf16(members, packed, LANES), in_s...  3.46 us
    ppermute x1, starting transfers between devices, per_device(): left = lax.ppermute(own, 'gx', up)  1.92 us
  transfers between devices with their start and end apart: 2, of which 2 were waited for; matrix products, arithmetic and copies ran while one was open for 1% of the time, Pallas kernels for 0%

profile of v2, /device:TPU:1, one launch (start us, length us, event | category | flops | bytes accessed | tf_op | source)
XLA Modules:
  0.0 59.7 jit_solution(14904877219157348586)
XLA Ops:
  0.0 0.0 copy-start
  0.0 0.7 %copy-done = bf16[2,16,160]{2,1,0:T(8,128)(2,1)S(1)} copy-done((bf16[2,16,160]{2,1,0:T(8,128)(2,1)S(1)}, bf16[2,16,160]{2,1,0:T(8,128)(2,1)}, u32[]{:S(2)}) %copy-start) | copy-done | bytes 10264
  0.7 0.1 pack.1
  0.8 0.0 copy-start.1
  0.8 19.0 %all_to_all.10.own_ref = bf16[16,40,128]{2,1,0:T(8,128)(2,1)S(1)} all-to-all(bf16[16,40,128]{2,1,0:T(8,128)(2,1)S(1)} %pack.1), channel_id=1, replica_groups=mesh['gx'=32,'gy'=2,'gz'=8] {'gy','gz'}, dimensions={0} | all-to-all | bytes 327680 | tf_op jit(solution)/shard_map/all_to_all | solution.py:138
  19.8 11.9 %collective-permute-start.1 = (bf16[16,40,128]{2,1,0:T(8,128)(2,1)S(1)}, bf16[16,40,128]{2,1,0:T(8,128)(2,1)S(1)}, u32[]{:S(2)}, u32[]{:S(2)}) collective-permute-start(bf16[16,40,128]{2,1,0:T(8,128)(2,1)S(1)} %all_to_all.10.own_ref), channel_id=1, source_target_pairs={{0,496},{16,0},{32,16},{48,32},{64,48},{80,64},{96,80},{112,96},{1... | collective-permute-start | bytes 491528 | tf_op jit(solution)/shard_map/ppermute | solution.py:140
  31.7 1.9 %collective-permute-start = (bf16[16,40,128]{2,1,0:T(8,128)(2,1)S(1)}, bf16[16,40,128]{2,1,0:T(8,128)(2,1)S(1)}, u32[]{:S(2)}, u32[]{:S(2)}) collective-permute-start(bf16[16,40,128]{2,1,0:T(8,128)(2,1)S(1)} %all_to_all.10.own_ref), channel_id=1, source_target_pairs={{0,16},{16,32},{32,48},{48,64},{64,80},{80,96},{96,112},{112,128},... | collective-permute-start | bytes 491528 | tf_op jit(solution)/shard_map/ppermute | solution.py:139
  34.3 0.8 %compare_select_fusion.2 = (s32[64]{0:T(128)S(1)}, s32[64]{0:T(128)S(1)}) fusion(s32[512]{0:T(512)} %param.9, s32[]{:T(128)S(6)} %select_n.31, s32[]{:T(128)} %bitcast.1, s32[]{:T(128)S(6)} %mul.16, s32[]{:T(128)S(6)} %axis_index.25, s32[512]{0:T(512)} %param.10), kind=kLoop, calls=%fused_computation.2 | loop fusion | flops 3712 | bytes 1040 | tf_op jit(solution)/shard_map/jit(_where)/select_n | solution.py:153
  35.1 0.4 collective-permute-done.1.right_ref
  35.5 7.2 %collective-permute-done.left_ref = bf16[16,40,128]{2,1,0:T(8,128)(2,1)S(1)} collective-permute-done((bf16[16,40,128]{2,1,0:T(8,128)(2,1)S(1)}, bf16[16,40,128]{2,1,0:T(8,128)(2,1)S(1)}, u32[]{:S(2)}, u32[]{:S(2)}) %collective-permute-start) | collective-permute-done | bytes 163872 | tf_op jit(solution)/shard_map/ppermute | solution.py:139
  42.6 3.5 %field.1 = bf16[16,40,128]{2,1,0:T(8,128)(2,1)S(1)} custom-call(s32[64]{0:T(128)S(1)} %get-tuple-element.6.start_ref, s32[64]{0:T(128)S(1)} %get-tuple-element.5.slot_ref, bf16[16,40,128]{2,1,0:T(8,128)(2,1)S(1)} %collective-permute-done.left_ref, bf16[16,40,128]{2,1,0:T(8,128)(2,1)S(1)} %all_to_all.10.own_ref, ...), custom_call_target="tpu_custom_call" | custom-call | tf_op jit(solution)/shard_map/field/pallas_call | solution.py:154
  46.1 12.9 %all_to_all.11.parts_ref = bf16[16,40,128]{2,1,0:T(8,128)(2,1)S(1)} all-to-all(bf16[16,40,128]{2,1,0:T(8,128)(2,1)S(1)} %field.1), channel_id=1, replica_groups=mesh['gx'=32,'gy'=2,'gz'=8] {'gy','gz'}, dimensions={0} | all-to-all | bytes 327680 | tf_op jit(solution)/shard_map/all_to_all | solution.py:172
  59.0 0.0 copy-done.1
  59.1 0.7 %final.1 = bf16[2,16,160]{2,1,0:T(8,128)(2,1)} custom-call(bf16[2,16,160]{2,1,0:T(8,128)(2,1)S(1)} %copy-done.1, bf16[16,40,128]{2,1,0:T(8,128)(2,1)S(1)} %all_to_all.11.parts_ref), custom_call_target="tpu_custom_call" | custom-call | tf_op jit(solution)/shard_map/final/pallas_call | solution.py:173
Async XLA Ops:
  0.0 0.7 %copy-start = (bf16[2,16,160]{2,1,0:T(8,128)(2,1)S(1)}, bf16[2,16,160]{2,1,0:T(8,128)(2,1)}, u32[]{:S(2)}) copy-start(bf16[2,16,160]{2,1,0:T(8,128)(2,1)} %x_ref.3) | copy-start | bytes 30724
  0.8 58.3 %copy-start.1 = (bf16[2,16,160]{2,1,0:T(8,128)(2,1)S(1)}, bf16[2,16,160]{2,1,0:T(8,128)(2,1)}, u32[]{:S(2)}) copy-start(bf16[2,16,160]{2,1,0:T(8,128)(2,1)} %x_ref.3) | copy-start | bytes 30724
  19.8 15.7 %collective-permute-start.1 = (bf16[16,40,128]{2,1,0:T(8,128)(2,1)S(1)}, bf16[16,40,128]{2,1,0:T(8,128)(2,1)S(1)}, u32[]{:S(2)}, u32[]{:S(2)}) collective-permute-start(bf16[16,40,128]{2,1,0:T(8,128)(2,1)S(1)} %all_to_all.10.own_ref), channel_id=1, source_target_pairs={{0,496},{16,0},{32,16},{48,32},{64,48},{80,64},{96,80},{112,96},{1... | collective-permute-start | bytes 491528 | tf_op jit(solution)/shard_map/ppermute | solution.py:140
  31.7 10.9 %collective-permute-start = (bf16[16,40,128]{2,1,0:T(8,128)(2,1)S(1)}, bf16[16,40,128]{2,1,0:T(8,128)(2,1)S(1)}, u32[]{:S(2)}, u32[]{:S(2)}) collective-permute-start(bf16[16,40,128]{2,1,0:T(8,128)(2,1)S(1)} %all_to_all.10.own_ref), channel_id=1, source_target_pairs={{0,16},{16,32},{32,48},{48,64},{64,80},{80,96},{96,112},{112,128},... | collective-permute-start | bytes 491528 | tf_op jit(solution)/shard_map/ppermute | solution.py:139

commit v3 on v2

v3 whole, which is shorter than its diff:
```python
import jax
import jax.numpy as jnp
from jax import lax
from jax.experimental import pallas as pl
from jax.experimental.pallas import tpu as pltpu
from jax.sharding import PartitionSpec as P


LANES = 128
COLUMN = ("gy", "gz")
CHUNKS = 4
VMEM = pl.BlockSpec(memory_space=pltpu.VMEM)
HBM = pl.BlockSpec(memory_space=pltpu.HBM)


def pack_rows(full, rest):
    quarter = full.shape[0] // 4
    lane = lax.broadcasted_iota(jnp.int32, (quarter, LANES), 1)
    packed = rest[:quarter]
    for q in range(1, 4):
        part = pltpu.roll(rest[q * quarter : (q + 1) * quarter], 32 * q, 1)
        packed = jnp.where(lane < 32 * q, packed, part)
    return jnp.concatenate([full, packed], axis=0)


def unpack_rest(packed):
    parts = [packed] + [pltpu.roll(packed, LANES - 32 * q, 1) for q in range(1, 4)]
    return jnp.concatenate(parts, axis=0)


def widen(value):
    rows = value.shape[0]
    return jnp.concatenate([value, jnp.zeros((rows, LANES - value.shape[1]), value.dtype)], axis=1)


def pack_kernel(x_ref, out_ref):
    rhs, spheres, length = x_ref.shape
    x = x_ref[...].astype(jnp.float32).reshape(rhs * spheres, length)
    packed = pack_rows(x[:, :LANES], widen(x[:, LANES:])).astype(jnp.bfloat16)
    for d in range(out_ref.shape[0]):
        out_ref[d] = packed


def contract_kernel(
    table_hbm, left_ref, own_ref, right_ref, mine_ref, other_hbm, near_out,
    table_ref, other_ref, full_ref, rest_ref, near_ref, sems,
):
    table_copy = pltpu.make_async_copy(table_hbm, table_ref, sems.at[0])
    table_copy.start()
    part = other_ref.shape[0] // CHUNKS
    copies = []
    for c in range(CHUNKS):
        at = pl.ds(c * part, part)
        copies.append(pltpu.make_async_copy(other_hbm.at[at], other_ref.at[at], sems.at[c + 1]))
        copies[c].start()
    slots = mine_ref.shape[0]
    spheres, rhs, _ = near_out.shape
    length = mine_ref.shape[2]
    members = own_ref.shape[0]
    rows = own_ref.shape[1] * LANES // length
    core = lax.rem(lax.axis_index("gz"), 2)
    for b, ref in enumerate((left_ref, own_ref, right_ref)):
        for d in range(members):
            at = (b * members + d) * rows
            piece = ref[d].astype(jnp.float32)
            full_ref[at : at + rows, :] = piece[:rows]
            rest_ref[at : at + rows, :] = unpack_rest(piece[rows:])
    near_ref[...] = jnp.zeros_like(near_ref)
    table_copy.wait()
    for ref, base in ((mine_ref, core * slots), (other_ref, (1 - core) * slots)):
        for p in range(slots):
            if ref is other_ref and p % part == 0:
                copies[p // part].wait()
            at = pl.ds(table_ref[0, base + p], rhs, stride=spheres // 2)
            x = jnp.concatenate([full_ref[at, :], rest_ref[at, :][:, : length - LANES]], axis=1)
            contrib = lax.dot_general(
                x.astype(jnp.bfloat16), ref[p], (((1,), (1,)), ((), ())),
                preferred_element_type=jnp.float32,
            )
            slot = table_ref[1, base + p]
            near_ref[slot] = near_ref[slot] + contrib
    near_out[...] = near_ref[:spheres].astype(jnp.bfloat16)


def apply_kernel(near_ref, tmat_ref, out_ref, full_ref, rest_ref):
    spheres, rhs, _ = near_ref.shape
    half = spheres // 2
    members = out_ref.shape[0]
    rows = full_ref.shape[0] // members
    for s in range(spheres):
        scattered = jnp.dot(near_ref[s], tmat_ref[s], preferred_element_type=jnp.float32)
        at = pl.ds((s // half) * rhs * half + s % half, rhs, stride=half)
        full_ref[at, :] = scattered[:, :LANES]
        rest_ref[at, :] = widen(scattered[:, LANES:])
    for d in range(members):
        at = slice(d * rows, (d + 1) * rows)
        out_ref[d] = pack_rows(full_ref[at, :], rest_ref[at, :]).astype(jnp.bfloat16)


def final_kernel(x_ref, parts_ref, out_ref):
    rhs, spheres, length = x_ref.shape
    rows = rhs * spheres
    total = parts_ref[0].astype(jnp.float32)
    for d in range(1, parts_ref.shape[0]):
        total = total + parts_ref[d].astype(jnp.float32)
    rest = unpack_rest(total[rows:])[:, : length - LANES]
    scattered = jnp.concatenate([total[:rows], rest], axis=1)
    x = x_ref[...].astype(jnp.float32).reshape(rows, length)
    out_ref[...] = (x - scattered).astype(jnp.bfloat16).reshape(rhs, spheres, length)


def limit(mebibytes):
    return pltpu.CompilerParams(vmem_limit_bytes=mebibytes * 2**20)


def cost(flops, size):
    return pl.CostEstimate(flops=flops, bytes_accessed=size, transcendentals=0)


def bf16(*shape):
    return jax.ShapeDtypeStruct(shape, jnp.bfloat16)


def per_device(coeffs, translations, tmatrix, pair_target, pair_source, pair_count):
    groups = lax.axis_size("gx")
    cores = 2
    members = lax.axis_size("gy") * lax.axis_size("gz") // cores
    rhs, spheres, length = coeffs.shape
    rows = rhs * spheres
    packed = rows * length // LANES
    slots, half_length, _ = translations.shape
    group_spheres = tmatrix.shape[0]
    rhs_core = rhs * lax.axis_size("gz") // cores
    up = [(g, (g + 1) % groups) for g in range(groups)]
    down = [(g, (g - 1) % groups) for g in range(groups)]
    sibling = [(i, i ^ 1) for i in range(lax.axis_size("gz"))]
    same_core = [[cores * y + c for y in range(members)] for c in range(cores)]

    def exchange(pieces):
        return lax.all_to_all(
            pieces, COLUMN, split_axis=0, concat_axis=0, tiled=True, axis_index_groups=same_core
        )

    shards = pl.pallas_call(
        pack_kernel, out_shape=bf16(members, packed, LANES), in_specs=[VMEM], out_specs=VMEM,
        compiler_params=limit(2), cost_estimate=cost(10**9, 2**18), name="pack",
    )(coeffs)
    other = lax.ppermute(translations, "gz", sibling)
    own = exchange(shards)
    left = lax.ppermute(own, "gx", up)
    right = lax.ppermute(own, "gx", down)
    base = lax.axis_index("gz") // cores * (cores * slots)
    source = lax.dynamic_slice_in_dim(pair_source, base, cores * slots)
    target = lax.dynamic_slice_in_dim(pair_target, base, cores * slots)
    relative = (source // group_spheres - lax.axis_index("gx") + 1 + groups) % groups
    sphere = source % group_spheres
    start = (relative * 2 + sphere // spheres) * (rhs_core * spheres) + sphere % spheres
    living = base + jnp.arange(cores * slots, dtype=jnp.int32) < pair_count[0]
    slot = jnp.where(living, target, group_spheres)
    window = pltpu.VMEM((3 * members * rows, LANES), jnp.float32)
    near = pl.pallas_call(
        contract_kernel,
        out_shape=bf16(group_spheres, rhs_core, half_length),
        in_specs=[HBM] + [VMEM] * 4 + [HBM],
        out_specs=VMEM,
        scratch_shapes=[
            pltpu.SMEM((2, cores * slots), jnp.int32),
            pltpu.VMEM(translations.shape, jnp.bfloat16),
            window,
            window,
            pltpu.VMEM((group_spheres + 1, rhs_core, half_length), jnp.float32),
            pltpu.SemaphoreType.DMA((CHUNKS + 1,)),
        ],
        compiler_params=limit(10),
        cost_estimate=cost(4 * rhs_core * translations.size, 4 * translations.size),
        name="contract",
    )(jnp.stack([start, slot]), left, own, right, translations, other)
    parts = pl.pallas_call(
        apply_kernel,
        out_shape=bf16(members, packed, LANES),
        in_specs=[VMEM] * 2,
        out_specs=VMEM,
        scratch_shapes=[pltpu.VMEM((members * rows, LANES), jnp.float32)] * 2,
        compiler_params=limit(4),
        cost_estimate=cost(2 * rhs_core * tmatrix.size, 2 * tmatrix.size),
        name="apply",
    )(near, tmatrix)
    arrived = exchange(parts)
    return pl.pallas_call(
        final_kernel, out_shape=bf16(*coeffs.shape), in_specs=[VMEM] * 2, out_specs=VMEM,
        compiler_params=limit(2), name="final",
    )(coeffs, arrived)


def solution(mesh):
    placed = (
        P("gz", ("gx", "gy"), None),
        P(("gx", "gz"), "gy", None),
        P("gx", "gy", None),
        P("gx"),
        P("gx"),
        P("gx"),
    )
    return jax.shard_map(
        per_device,
        mesh=mesh,
        in_specs=placed,
        out_specs=P("gz", ("gx", "gy"), None),
        check_vma=False,
    )
```

time: 60.1 us -> 56.3 us (0.937)
  the two profiles are of different devices: /device:TPU:1 before, /device:TPU:8 now
where the time goes in v3:
time: 56.3 us; the launch traced here: 55.8 us
  starting transfers between devices  24.5 us (44%)
  waiting for transfers between devices  13.8 us (25%)
  blocking collectives  10.9 us (19%)
  Pallas kernels  4.42 us (8%)
  other arithmetic  0.8 us (1%)
  local copies, waits for them, and re-layouts  0.73 us (1%)
  between operations  0.73 us (1%)
    ppermute x1, starting transfers between devices, per_device(): right = lax.ppermute(own, 'gx', down)  11.3 us
    all_to_all x1, blocking collectives, exchange(): lax.all_to_all(pieces, COLUMN, split_axis=0, concat_axis=0, tiled=True, a...  10.9 us
    all_to_all x1, starting transfers between devices, exchange(): lax.all_to_all(pieces, COLUMN, split_axis=0, concat_axis=0, tiled=True, a...  9.05 us
    ppermute x1, waiting for transfers between devices, per_device(): left = lax.ppermute(own, 'gx', up)  7.62 us
    all_to_all x1, waiting for transfers between devices, exchange(): lax.all_to_all(pieces, COLUMN, split_axis=0, concat_axis=0, tiled=True, a...  6.08 us
    pallas_call x1, Pallas kernels, per_device(): pl.pallas_call(contract_kernel, out_shape=bf16(group_spheres, rhs_core, h...  2.64 us
    ppermute x1, starting transfers between devices, per_device(): other = lax.ppermute(translations, 'gz', sibling)  2.17 us
    ppermute x1, starting transfers between devices, per_device(): left = lax.ppermute(own, 'gx', up)  1.92 us
  transfers between devices with their start and end apart: 4, of which 3 were waited for; matrix products, arithmetic and copies ran while one was open for 1% of the time, Pallas kernels for 1%

profile of v3, /device:TPU:8, one launch (start us, length us, event | category | flops | bytes accessed | tf_op | source)
XLA Modules:
  0.0 55.8 jit_solution(15060051882802153759)
XLA Ops:
  0.0 0.0 copy-start
  0.0 2.2 %collective-permute-start.2 = (bf16[64,80,160]{2,1,0:T(8,128)(2,1)}, bf16[64,80,160]{2,1,0:T(8,128)(2,1)}, u32[]{:S(2)}, u32[]{:S(2)}) collective-permute-start(bf16[64,80,160]{2,1,0:T(8,128)(2,1)} %mine_ref.1), channel_id=1, source_target_pairs={{0,1},{1,0},{2,3},{3,2},{4,5},{5,4},{6,7},{7,6},{8,9},{9,8},{10,11... | collective-permute-start | bytes 4915208 | tf_op jit(solution)/shard_map/ppermute | solution.py:148
  2.2 0.0 copy-start.2
  2.2 0.7 %copy-done.2 = bf16[2,16,160]{2,1,0:T(8,128)(2,1)S(1)} copy-done((bf16[2,16,160]{2,1,0:T(8,128)(2,1)S(1)}, bf16[2,16,160]{2,1,0:T(8,128)(2,1)}, u32[]{:S(2)}) %copy-start.2) | copy-done | bytes 10264
  2.9 0.7 %pack.1 = bf16[8,40,128]{2,1,0:T(8,128)(2,1)} custom-call(bf16[2,16,160]{2,1,0:T(8,128)(2,1)S(1)} %copy-done.2), custom_call_target="tpu_custom_call" | custom-call | flops 1000000000 | bytes 262144 | tf_op jit(solution)/shard_map/pack/pallas_call | solution.py:144
  3.6 9.1 %all-to-all-start = ((bf16[8,40,128]{2,1,0:T(8,128)(2,1)}), bf16[8,40,128]{2,1,0:T(8,128)(2,1)S(1)}, u32[]{:S(2)}, u32[]{:S(2)}) async-start(bf16[8,40,128]{2,1,0:T(8,128)(2,1)} %pack.1), calls=%async_computation | async-start | bytes 163840 | tf_op jit(solution)/shard_map/all_to_all | solution.py:140
  13.3 0.8 %fusion.3 = (s32[1,128]{1,0:T(1,128)S(1)}, s32[1,128]{1,0:T(1,128)S(1)}) fusion(s32[512]{0:T(512)} %param.9, s32[]{:T(128)S(6)} %select_n.36, s32[]{:T(128)} %bitcast.5, s32[]{:T(128)S(6)} %mul.15, s32[]{:T(128)S(6)} %axis_index.25, s32[512]{0:T(512)} %param.10), kind=kLoop, calls=%fused_computation.18 | loop fusion | flops 7424 | bytes 2064 | tf_op jit(solution)/shard_map/stack | solution.py:177
  14.1 6.1 %all-to-all-done.own_ref = bf16[8,40,128]{2,1,0:T(8,128)(2,1)S(1)} async-done(((bf16[8,40,128]{2,1,0:T(8,128)(2,1)}), bf16[8,40,128]{2,1,0:T(8,128)(2,1)S(1)}, u32[]{:S(2)}, u32[]{:S(2)}) %all-to-all-start) | async-done | bytes 81952 | tf_op jit(solution)/shard_map/all_to_all | solution.py:140
  20.2 11.3 %collective-permute-start.1 = (bf16[8,40,128]{2,1,0:T(8,128)(2,1)S(1)}, bf16[8,40,128]{2,1,0:T(8,128)(2,1)S(1)}, u32[]{:S(2)}, u32[]{:S(2)}) collective-permute-start(bf16[8,40,128]{2,1,0:T(8,128)(2,1)S(1)} %all-to-all-done.own_ref), channel_id=1, source_target_pairs={{0,496},{16,0},{32,16},{48,32},{64,48},{80,64},{96,80},{112,96},{1... | collective-permute-start | bytes 245768 | tf_op jit(solution)/shard_map/ppermute | solution.py:151
  31.5 1.9 %collective-permute-start = (bf16[8,40,128]{2,1,0:T(8,128)(2,1)S(1)}, bf16[8,40,128]{2,1,0:T(8,128)(2,1)S(1)}, u32[]{:S(2)}, u32[]{:S(2)}) collective-permute-start(bf16[8,40,128]{2,1,0:T(8,128)(2,1)S(1)} %all-to-all-done.own_ref), channel_id=1, source_target_pairs={{0,16},{16,32},{32,48},{48,64},{64,80},{80,96},{96,112},{112,128},... | collective-permute-start | bytes 245768 | tf_op jit(solution)/shard_map/ppermute | solution.py:150
  33.5 0.0 copy-start.1
  33.5 0.0 copy-start.3
  33.5 0.1 collective-permute-done.1.right_ref
  33.6 7.6 %collective-permute-done.left_ref = bf16[8,40,128]{2,1,0:T(8,128)(2,1)S(1)} collective-permute-done((bf16[8,40,128]{2,1,0:T(8,128)(2,1)S(1)}, bf16[8,40,128]{2,1,0:T(8,128)(2,1)S(1)}, u32[]{:S(2)}, u32[]{:S(2)}) %collective-permute-start) | collective-permute-done | bytes 81952 | tf_op jit(solution)/shard_map/ppermute | solution.py:150
  41.2 0.0 collective-permute-done.2.other_hbm
  41.2 0.0 copy-done
  41.2 2.6 %contract.1.near_ref = bf16[32,8,80]{2,1,0:T(8,128)(2,1)S(1)} custom-call(s32[2,128]{1,0:T(2,128)S(1)} %pad_add_fusion.table_hbm, bf16[8,40,128]{2,1,0:T(8,128)(2,1)S(1)} %collective-permute-done.left_ref, bf16[8,40,128]{2,1,0:T(8,128)(2,1)S(1)} %all-to-all-done.own_ref, bf16[8,40,128]{2,1,0:T(8,128)(2,1)S(1)} %collective-permute-done.1.right_ref, ...), custom_call_target="tpu_custom_call" | custom-call | flops 26214400 | bytes 3276800 | tf_op jit(solution)/shard_map/contract/pallas_call | solution.py:161
  43.8 0.0 copy-done.1
  43.9 0.4 apply.1
  44.2 10.9 %all_to_all.10.parts_ref = bf16[8,40,128]{2,1,0:T(8,128)(2,1)S(1)} all-to-all(bf16[8,40,128]{2,1,0:T(8,128)(2,1)S(1)} %apply.1), channel_id=1, replica_groups={{0,2,4,6,8,10,12,14},{1,3,5,7,9,11,13,15},{16,18,20,22,24,26,28,30},{17..., dimensions={0} | all-to-all | bytes 163840 | tf_op jit(solution)/shard_map/all_to_all | solution.py:140
  55.1 0.0 copy-done.3
  55.1 0.7 %final.1 = bf16[2,16,160]{2,1,0:T(8,128)(2,1)} custom-call(bf16[2,16,160]{2,1,0:T(8,128)(2,1)S(1)} %copy-done.3, bf16[8,40,128]{2,1,0:T(8,128)(2,1)S(1)} %all_to_all.10.parts_ref), custom_call_target="tpu_custom_call" | custom-call | tf_op jit(solution)/shard_map/final/pallas_call | solution.py:189
  (1 shorter events, 0.0 us)
Async XLA Ops:
  0.0 41.2 %copy-start = (bf16[64,80,160]{2,1,0:T(8,128)(2,1)S(1)}, bf16[64,80,160]{2,1,0:T(8,128)(2,1)}, u32[]{:S(2)}) copy-start(bf16[64,80,160]{2,1,0:T(8,128)(2,1)} %mine_ref.1) | copy-start | bytes 4915204
  0.0 41.2 %collective-permute-start.2 = (bf16[64,80,160]{2,1,0:T(8,128)(2,1)}, bf16[64,80,160]{2,1,0:T(8,128)(2,1)}, u32[]{:S(2)}, u32[]{:S(2)}) collective-permute-start(bf16[64,80,160]{2,1,0:T(8,128)(2,1)} %mine_ref.1), channel_id=1, source_target_pairs={{0,1},{1,0},{2,3},{3,2},{4,5},{5,4},{6,7},{7,6},{8,9},{9,8},{10,11... | collective-permute-start | bytes 4915208 | tf_op jit(solution)/shard_map/ppermute | solution.py:148
  2.2 0.7 %copy-start.2 = (bf16[2,16,160]{2,1,0:T(8,128)(2,1)S(1)}, bf16[2,16,160]{2,1,0:T(8,128)(2,1)}, u32[]{:S(2)}) copy-start(bf16[2,16,160]{2,1,0:T(8,128)(2,1)} %x_ref.3) | copy-start | bytes 30724
  3.6 16.6 %all-to-all-start = ((bf16[8,40,128]{2,1,0:T(8,128)(2,1)}), bf16[8,40,128]{2,1,0:T(8,128)(2,1)S(1)}, u32[]{:S(2)}, u32[]{:S(2)}) async-start(bf16[8,40,128]{2,1,0:T(8,128)(2,1)} %pack.1), calls=%async_computation | async-start | bytes 163840 | tf_op jit(solution)/shard_map/all_to_all | solution.py:140
  20.2 13.4 %collective-permute-start.1 = (bf16[8,40,128]{2,1,0:T(8,128)(2,1)S(1)}, bf16[8,40,128]{2,1,0:T(8,128)(2,1)S(1)}, u32[]{:S(2)}, u32[]{:S(2)}) collective-permute-start(bf16[8,40,128]{2,1,0:T(8,128)(2,1)S(1)} %all-to-all-done.own_ref), channel_id=1, source_target_pairs={{0,496},{16,0},{32,16},{48,32},{64,48},{80,64},{96,80},{112,96},{1... | collective-permute-start | bytes 245768 | tf_op jit(solution)/shard_map/ppermute | solution.py:151
  31.5 9.7 %collective-permute-start = (bf16[8,40,128]{2,1,0:T(8,128)(2,1)S(1)}, bf16[8,40,128]{2,1,0:T(8,128)(2,1)S(1)}, u32[]{:S(2)}, u32[]{:S(2)}) collective-permute-start(bf16[8,40,128]{2,1,0:T(8,128)(2,1)S(1)} %all-to-all-done.own_ref), channel_id=1, source_target_pairs={{0,16},{16,32},{32,48},{48,64},{64,80},{80,96},{96,112},{112,128},... | collective-permute-start | bytes 245768 | tf_op jit(solution)/shard_map/ppermute | solution.py:150
  33.5 10.4 %copy-start.1 = (bf16[32,80,160]{2,1,0:T(8,128)(2,1)S(1)}, bf16[32,80,160]{2,1,0:T(8,128)(2,1)}, u32[]{:S(2)}) copy-start(bf16[32,80,160]{2,1,0:T(8,128)(2,1)} %tmat_ref.1) | copy-start | bytes 2457604
  33.5 21.7 %copy-start.3 = (bf16[2,16,160]{2,1,0:T(8,128)(2,1)S(1)}, bf16[2,16,160]{2,1,0:T(8,128)(2,1)}, u32[]{:S(2)}) copy-start(bf16[2,16,160]{2,1,0:T(8,128)(2,1)} %x_ref.3) | copy-start | bytes 30724

commit v4 on v3

--- a/solution.py
+++ b/solution.py
@@ -7,10 +7,11 @@
 
 
 LANES = 128
+RUN = 8
 COLUMN = ("gy", "gz")
-CHUNKS = 4
 VMEM = pl.BlockSpec(memory_space=pltpu.VMEM)
 HBM = pl.BlockSpec(memory_space=pltpu.HBM)
+SMEM = pl.BlockSpec(memory_space=pltpu.SMEM)
 
 
 def pack_rows(full, rest):
@@ -33,7 +34,8 @@
     return jnp.concatenate([value, jnp.zeros((rows, LANES - value.shape[1]), value.dtype)], axis=1)
 
 
-def pack_kernel(x_ref, out_ref):
+def pack_kernel(count_ref, x_ref, out_ref):
+    del count_ref
     rhs, spheres, length = x_ref.shape
     x = x_ref[...].astype(jnp.float32).reshape(rhs * spheres, length)
     packed = pack_rows(x[:, :LANES], widen(x[:, LANES:])).astype(jnp.bfloat16)
@@ -42,42 +44,50 @@
 
 
 def contract_kernel(
-    table_hbm, left_ref, own_ref, right_ref, mine_ref, other_hbm, near_out,
-    table_ref, other_ref, full_ref, rest_ref, near_ref, sems,
+    count_ref, source_hbm, target_hbm, own_ref, odd_ref, even_ref, even_last_ref, mine_ref, other_ref, near_out,
+    source_ref, target_ref, full_ref, rest_ref, near_ref, sems,
 ):
-    table_copy = pltpu.make_async_copy(table_hbm, table_ref, sems.at[0])
-    table_copy.start()
-    part = other_ref.shape[0] // CHUNKS
-    copies = []
-    for c in range(CHUNKS):
-        at = pl.ds(c * part, part)
-        copies.append(pltpu.make_async_copy(other_hbm.at[at], other_ref.at[at], sems.at[c + 1]))
-        copies[c].start()
+    here = lax.axis_index("gx")
+    groups = lax.axis_size("gx")
+    core = lax.rem(lax.axis_index("gz"), 2)
+    base = pl.multiple_of((lax.axis_index("gz") - core) * mine_ref.shape[0], LANES)
+    tables = []
+    for i, (hbm, ref) in enumerate(((source_hbm, source_ref), (target_hbm, target_ref))):
+        tables.append(pltpu.make_async_copy(hbm.at[pl.ds(base, ref.shape[0])], ref, sems.at[i]))
+        tables[i].start()
     slots = mine_ref.shape[0]
     spheres, rhs, _ = near_out.shape
     length = mine_ref.shape[2]
     members = own_ref.shape[0]
     rows = own_ref.shape[1] * LANES // length
-    core = lax.rem(lax.axis_index("gz"), 2)
-    for b, ref in enumerate((left_ref, own_ref, right_ref)):
+    odd_block = 2 * lax.rem(here, 2)
+    for ref, block in ((own_ref, 1), (odd_ref, odd_block), (even_ref, 2 - odd_block)):
         for d in range(members):
-            at = (b * members + d) * rows
+            at = pl.ds(pl.multiple_of((block * members + d) * rows, rows), rows)
             piece = ref[d].astype(jnp.float32)
-            full_ref[at : at + rows, :] = piece[:rows]
-            rest_ref[at : at + rows, :] = unpack_rest(piece[rows:])
+            if ref is even_ref:
+                piece = piece + even_last_ref[d].astype(jnp.float32)
+            full_ref[at, :] = piece[:rows]
+            rest_ref[at, :] = unpack_rest(piece[rows:])
     near_ref[...] = jnp.zeros_like(near_ref)
-    table_copy.wait()
-    for ref, base in ((mine_ref, core * slots), (other_ref, (1 - core) * slots)):
+    for copy in tables:
+        copy.wait()
+    half = spheres // 2
+    assert half & (half - 1) == 0 and groups & (groups - 1) == 0
+    shift = half.bit_length() - 1
+    offset = (1 - here + groups) * spheres
+    live = count_ref[0] - base
+    for ref, first in ((mine_ref, core * slots), (other_ref, (1 - core) * slots)):
         for p in range(slots):
-            if ref is other_ref and p % part == 0:
-                copies[p // part].wait()
-            at = pl.ds(table_ref[0, base + p], rhs, stride=spheres // 2)
+            near_by = (source_ref[first + p] + offset) & (groups * spheres - 1)
+            start = lax.shift_right_logical(near_by, shift) * (rhs * half) + (near_by & (half - 1))
+            at = pl.ds(start, rhs, stride=half)
             x = jnp.concatenate([full_ref[at, :], rest_ref[at, :][:, : length - LANES]], axis=1)
             contrib = lax.dot_general(
                 x.astype(jnp.bfloat16), ref[p], (((1,), (1,)), ((), ())),
                 preferred_element_type=jnp.float32,
             )
-            slot = table_ref[1, base + p]
+            slot = jnp.where(first + p < live, target_ref[first + p], spheres)
             near_ref[slot] = near_ref[slot] + contrib
     near_out[...] = near_ref[:spheres].astype(jnp.bfloat16)
 
@@ -131,8 +141,8 @@
     slots, half_length, _ = translations.shape
     group_spheres = tmatrix.shape[0]
     rhs_core = rhs * lax.axis_size("gz") // cores
-    up = [(g, (g + 1) % groups) for g in range(groups)]
-    down = [(g, (g - 1) % groups) for g in range(groups)]
+    even_pairs = [(g, g ^ 1) for g in range(groups)]
+    odd_pairs = [(g, (g + 1 if g % 2 else g - 1) % groups) for g in range(groups)]
     sibling = [(i, i ^ 1) for i in range(lax.axis_size("gz"))]
     same_core = [[cores * y + c for y in range(members)] for c in range(cores)]
 
@@ -142,39 +152,32 @@
         )
 
     shards = pl.pallas_call(
-        pack_kernel, out_shape=bf16(members, packed, LANES), in_specs=[VMEM], out_specs=VMEM,
+        pack_kernel, out_shape=bf16(members, packed, LANES), in_specs=[SMEM, VMEM], out_specs=VMEM,
         compiler_params=limit(2), cost_estimate=cost(10**9, 2**18), name="pack",
-    )(coeffs)
+    )(pair_count, coeffs)
     other = lax.ppermute(translations, "gz", sibling)
     own = exchange(shards)
-    left = lax.ppermute(own, "gx", up)
-    right = lax.ppermute(own, "gx", down)
-    base = lax.axis_index("gz") // cores * (cores * slots)
-    source = lax.dynamic_slice_in_dim(pair_source, base, cores * slots)
-    target = lax.dynamic_slice_in_dim(pair_target, base, cores * slots)
-    relative = (source // group_spheres - lax.axis_index("gx") + 1 + groups) % groups
-    sphere = source % group_spheres
-    start = (relative * 2 + sphere // spheres) * (rhs_core * spheres) + sphere % spheres
-    living = base + jnp.arange(cores * slots, dtype=jnp.int32) < pair_count[0]
-    slot = jnp.where(living, target, group_spheres)
+    even_first = lax.ppermute(own, "gx", [p for p in even_pairs if p[0] % RUN < RUN - 2])
+    odd = lax.ppermute(own, "gx", odd_pairs)
+    even_last = lax.ppermute(own, "gx", [p for p in even_pairs if p[0] % RUN >= RUN - 2])
     window = pltpu.VMEM((3 * members * rows, LANES), jnp.float32)
     near = pl.pallas_call(
         contract_kernel,
         out_shape=bf16(group_spheres, rhs_core, half_length),
-        in_specs=[HBM] + [VMEM] * 4 + [HBM],
+        in_specs=[SMEM] + [HBM] * 2 + [VMEM] * 6,
         out_specs=VMEM,
         scratch_shapes=[
-            pltpu.SMEM((2, cores * slots), jnp.int32),
-            pltpu.VMEM(translations.shape, jnp.bfloat16),
+            pltpu.SMEM((cores * slots,), jnp.int32),
+            pltpu.SMEM((cores * slots,), jnp.int32),
             window,
             window,
             pltpu.VMEM((group_spheres + 1, rhs_core, half_length), jnp.float32),
-            pltpu.SemaphoreType.DMA((CHUNKS + 1,)),
+            pltpu.SemaphoreType.DMA((2,)),
         ],
         compiler_params=limit(10),
         cost_estimate=cost(4 * rhs_core * translations.size, 4 * translations.size),
         name="contract",
-    )(jnp.stack([start, slot]), left, own, right, translations, other)
+    )(pair_count, pair_source, pair_target, own, odd, even_first, even_last, translations, other)
     parts = pl.pallas_call(
         apply_kernel,
         out_shape=bf16(members, packed, LANES),

time: 56.3 us -> 51.6 us (0.917)
  blocking collectives: 10.9 us -> 26.6 us
  waiting for transfers between devices: 13.8 us -> 2.39 us
  starting transfers between devices: 24.5 us -> 17.5 us
  Pallas kernels: 4.42 us -> 3.34 us
  other arithmetic: 0.8 us -> 0 us
    all_to_all x1 -> x2, blocking collectives: 10.9 us -> 26.6 us  [exchange(): lax.all_to_all(pieces, COLUMN, split_axis=0, concat_axis=0, tiled=True, a...]
    all_to_all x1 -> x0, starting transfers between devices: 9.05 us -> none  [exchange(): lax.all_to_all(pieces, COLUMN, split_axis=0, concat_axis=0, tiled=True, a...]
    all_to_all x1 -> x0, waiting for transfers between devices: 6.08 us -> none  [exchange(): lax.all_to_all(pieces, COLUMN, split_axis=0, concat_axis=0, tiled=True, a...]
    ppermute x2 -> x3, waiting for transfers between devices: 7.69 us -> 2.39 us  [the longest x1 2.38 us: per_device(): odd = lax.ppermute(own, 'gx', odd_pairs)]
    ppermute x2 -> x3, starting transfers between devices: 13.2 us -> 15.3 us  [the longest x1 11.3 us: per_device(): odd = lax.ppermute(own, 'gx', odd_pairs)]
    another operation x2 -> x0, other arithmetic: 0.8 us -> none  [per_device(): jnp.stack([start, slot])]
    pallas_call x1, Pallas kernels: 0.72 us -> 0.08 us  [per_device(): pl.pallas_call(pack_kernel, out_shape=bf16(members, packed, LANES), in_sp...]
  transfers between devices with their start and end apart: 4 -> 4, of which waited for: 3 -> 1; matrix products, arithmetic and copies ran while one was open for 1% -> 0% of each run, Pallas kernels for 1% -> 0%
where the time goes in v4:
time: 51.6 us; the launch traced here: 51.2 us
  blocking collectives  26.6 us (52%)
  starting transfers between devices  17.5 us (34%)
  Pallas kernels  3.34 us (6%)
  waiting for transfers between devices  2.39 us (5%)
  local copies, waits for them, and re-layouts  0.73 us (1%)
  between operations  0.73 us (1%)
    all_to_all x2, blocking collectives, exchange(): lax.all_to_all(pieces, COLUMN, split_axis=0, concat_axis=0, tiled=True, a...  26.6 us
    ppermute x1, starting transfers between devices, per_device(): odd = lax.ppermute(own, 'gx', odd_pairs)  11.3 us
    ppermute x1, starting transfers between devices, per_device(): lax.ppermute(own, 'gx', [p for p in even_pairs if p[0] % RUN < RUN - 2])  3.18 us
    ppermute x1, waiting for transfers between devices, per_device(): odd = lax.ppermute(own, 'gx', odd_pairs)  2.38 us
    pallas_call x1, Pallas kernels, per_device(): pl.pallas_call(contract_kernel, out_shape=bf16(group_spheres, rhs_core, h...  2.2 us
    ppermute x1, starting transfers between devices, per_device(): other = lax.ppermute(translations, 'gz', sibling)  2.17 us
  transfers between devices with their start and end apart: 4, of which 1 were waited for; matrix products, arithmetic and copies ran while one was open for 0% of the time, Pallas kernels for 0%

profile of v4, /device:TPU:8, one launch (start us, length us, event | category | flops | bytes accessed | tf_op | source)
XLA Modules:
  0.0 51.2 jit_solution(5919802352250361650)
XLA Ops:
  0.0 0.0 copy-start
  0.0 2.2 %collective-permute-start.3 = (bf16[64,80,160]{2,1,0:T(8,128)(2,1)}, bf16[64,80,160]{2,1,0:T(8,128)(2,1)S(1)}, u32[]{:S(2)}, u32[]{:S(2)}) collective-permute-start(bf16[64,80,160]{2,1,0:T(8,128)(2,1)} %mine_ref.1), channel_id=1, source_target_pairs={{0,1},{1,0},{2,3},{3,2},{4,5},{5,4},{6,7},{7,6},{8,9},{9,8},{10,11... | collective-permute-start | bytes 4915208 | tf_op jit(solution)/shard_map/ppermute | solution.py:158
  2.8 0.0 copy-start.2
  2.8 0.7 %copy-done.2 = bf16[2,16,160]{2,1,0:T(8,128)(2,1)S(1)} copy-done((bf16[2,16,160]{2,1,0:T(8,128)(2,1)S(1)}, bf16[2,16,160]{2,1,0:T(8,128)(2,1)}, u32[]{:S(2)}) %copy-start.2) | copy-done | bytes 10264
  3.5 0.0 copy-start.3
  3.5 0.0 copy-start.4
  3.5 0.1 pack.1
  3.6 15.7 %all_to_all.10.own_ref = bf16[8,40,128]{2,1,0:T(8,128)(2,1)S(1)} all-to-all(bf16[8,40,128]{2,1,0:T(8,128)(2,1)S(1)} %pack.1), channel_id=1, replica_groups={{0,2,4,6,8,10,12,14},{1,3,5,7,9,11,13,15},{16,18,20,22,24,26,28,30},{17..., dimensions={0} | all-to-all | bytes 163840 | tf_op jit(solution)/shard_map/all_to_all | solution.py:150
  19.3 0.0 copy-start.1
  19.3 0.8 %collective-permute-start.2 = (bf16[8,40,128]{2,1,0:T(8,128)(2,1)S(1)}, bf16[8,40,128]{2,1,0:T(8,128)(2,1)S(1)}, u32[]{:S(2)}, u32[]{:S(2)}) collective-permute-start(bf16[8,40,128]{2,1,0:T(8,128)(2,1)S(1)} %all_to_all.10.own_ref), channel_id=1, source_target_pairs={{96,112},{112,96},{224,240},{240,224},{352,368},{368,352},{480,496... | collective-permute-start | bytes 245768 | tf_op jit(solution)/shard_map/ppermute | solution.py:162
  20.1 3.2 %collective-permute-start.1 = (bf16[8,40,128]{2,1,0:T(8,128)(2,1)S(1)}, bf16[8,40,128]{2,1,0:T(8,128)(2,1)S(1)}, u32[]{:S(2)}, u32[]{:S(2)}) collective-permute-start(bf16[8,40,128]{2,1,0:T(8,128)(2,1)S(1)} %all_to_all.10.own_ref), channel_id=1, source_target_pairs={{0,16},{16,0},{32,48},{48,32},{64,80},{80,64},{128,144},{144,128},... | collective-permute-start | bytes 245768 | tf_op jit(solution)/shard_map/ppermute | solution.py:160
  23.3 11.3 %collective-permute-start = (bf16[8,40,128]{2,1,0:T(8,128)(2,1)S(1)}, bf16[8,40,128]{2,1,0:T(8,128)(2,1)S(1)}, u32[]{:S(2)}, u32[]{:S(2)}) collective-permute-start(bf16[8,40,128]{2,1,0:T(8,128)(2,1)S(1)} %all_to_all.10.own_ref), channel_id=1, source_target_pairs={{0,496},{16,32},{32,16},{48,64},{64,48},{80,96},{96,80},{112,128},... | collective-permute-start | bytes 245768 | tf_op jit(solution)/shard_map/ppermute | solution.py:161
  34.6 0.0 collective-permute-done.2.even_last_ref
  34.6 0.0 collective-permute-done.1.even_ref
  34.6 2.4 %collective-permute-done.odd_ref = bf16[8,40,128]{2,1,0:T(8,128)(2,1)S(1)} collective-permute-done((bf16[8,40,128]{2,1,0:T(8,128)(2,1)S(1)}, bf16[8,40,128]{2,1,0:T(8,128)(2,1)S(1)}, u32[]{:S(2)}, u32[]{:S(2)}) %collective-permute-start) | collective-permute-done | bytes 81952 | tf_op jit(solution)/shard_map/ppermute | solution.py:161
  37.0 0.0 collective-permute-done.3.other_ref
  37.0 0.0 copy-done
  37.0 0.0 copy-done.3
  37.0 0.0 copy-done.4
  37.0 2.2 %contract.1.near_ref = bf16[32,8,80]{2,1,0:T(8,128)(2,1)S(1)} custom-call(s32[1]{0:T(128)S(6)} %copy.7.count_ref, s32[512]{0:T(512)S(1)} %copy-done.3, s32[512]{0:T(512)S(1)} %copy-done.4, bf16[8,40,128]{2,1,0:T(8,128)(2,1)S(1)} %all_to_all.10.own_ref, bf16[8,40,128]{2,1,0:T(8,128)(2,1)S(1)} %collective-permute-done.odd_ref, ...), custom_call_target="tpu_custom_call" | custom-call | flops 26214400 | bytes 3276800 | tf_op jit(solution)/shard_map/contract/pallas_call | solution.py:164
  39.2 0.0 copy-done.1
  39.2 0.4 apply.1
  39.6 10.9 %all_to_all.11.parts_ref = bf16[8,40,128]{2,1,0:T(8,128)(2,1)S(1)} all-to-all(bf16[8,40,128]{2,1,0:T(8,128)(2,1)S(1)} %apply.1), channel_id=1, replica_groups={{0,2,4,6,8,10,12,14},{1,3,5,7,9,11,13,15},{16,18,20,22,24,26,28,30},{17..., dimensions={0} | all-to-all | bytes 163840 | tf_op jit(solution)/shard_map/all_to_all | solution.py:150
  50.5 0.7 %final.1 = bf16[2,16,160]{2,1,0:T(8,128)(2,1)} custom-call(bf16[2,16,160]{2,1,0:T(8,128)(2,1)S(1)} %copy-done.2, bf16[8,40,128]{2,1,0:T(8,128)(2,1)S(1)} %all_to_all.11.parts_ref), custom_call_target="tpu_custom_call" | custom-call | tf_op jit(solution)/shard_map/final/pallas_call | solution.py:192
Async XLA Ops:
  0.0 37.0 %copy-start = (bf16[64,80,160]{2,1,0:T(8,128)(2,1)S(1)}, bf16[64,80,160]{2,1,0:T(8,128)(2,1)}, u32[]{:S(2)}) copy-start(bf16[64,80,160]{2,1,0:T(8,128)(2,1)} %mine_ref.1) | copy-start | bytes 4915204
  0.0 37.0 %collective-permute-start.3 = (bf16[64,80,160]{2,1,0:T(8,128)(2,1)}, bf16[64,80,160]{2,1,0:T(8,128)(2,1)S(1)}, u32[]{:S(2)}, u32[]{:S(2)}) collective-permute-start(bf16[64,80,160]{2,1,0:T(8,128)(2,1)} %mine_ref.1), channel_id=1, source_target_pairs={{0,1},{1,0},{2,3},{3,2},{4,5},{5,4},{6,7},{7,6},{8,9},{9,8},{10,11... | collective-permute-start | bytes 4915208 | tf_op jit(solution)/shard_map/ppermute | solution.py:158
  2.8 0.7 %copy-start.2 = (bf16[2,16,160]{2,1,0:T(8,128)(2,1)S(1)}, bf16[2,16,160]{2,1,0:T(8,128)(2,1)}, u32[]{:S(2)}) copy-start(bf16[2,16,160]{2,1,0:T(8,128)(2,1)} %x_ref.3) | copy-start | bytes 30724
  3.5 33.5 %copy-start.3 = (s32[512]{0:T(512)S(1)}, s32[512]{0:T(512)}, u32[]{:S(2)}) copy-start(s32[512]{0:T(512)} %source_hbm.1) | copy-start | bytes 6148
  3.5 33.5 %copy-start.4 = (s32[512]{0:T(512)S(1)}, s32[512]{0:T(512)}, u32[]{:S(2)}) copy-start(s32[512]{0:T(512)} %target_hbm.1) | copy-start | bytes 6148
  19.3 19.9 %copy-start.1 = (bf16[32,80,160]{2,1,0:T(8,128)(2,1)S(1)}, bf16[32,80,160]{2,1,0:T(8,128)(2,1)}, u32[]{:S(2)}) copy-start(bf16[32,80,160]{2,1,0:T(8,128)(2,1)} %tmat_ref.1) | copy-start | bytes 2457604
  19.3 15.3 %collective-permute-start.2 = (bf16[8,40,128]{2,1,0:T(8,128)(2,1)S(1)}, bf16[8,40,128]{2,1,0:T(8,128)(2,1)S(1)}, u32[]{:S(2)}, u32[]{:S(2)}) collective-permute-start(bf16[8,40,128]{2,1,0:T(8,128)(2,1)S(1)} %all_to_all.10.own_ref), channel_id=1, source_target_pairs={{96,112},{112,96},{224,240},{240,224},{352,368},{368,352},{480,496... | collective-permute-start | bytes 245768 | tf_op jit(solution)/shard_map/ppermute | solution.py:162
  20.1 14.5 %collective-permute-start.1 = (bf16[8,40,128]{2,1,0:T(8,128)(2,1)S(1)}, bf16[8,40,128]{2,1,0:T(8,128)(2,1)S(1)}, u32[]{:S(2)}, u32[]{:S(2)}) collective-permute-start(bf16[8,40,128]{2,1,0:T(8,128)(2,1)S(1)} %all_to_all.10.own_ref), channel_id=1, source_target_pairs={{0,16},{16,0},{32,48},{48,32},{64,80},{80,64},{128,144},{144,128},... | collective-permute-start | bytes 245768 | tf_op jit(solution)/shard_map/ppermute | solution.py:160
  23.3 13.7 %collective-permute-start = (bf16[8,40,128]{2,1,0:T(8,128)(2,1)S(1)}, bf16[8,40,128]{2,1,0:T(8,128)(2,1)S(1)}, u32[]{:S(2)}, u32[]{:S(2)}) collective-permute-start(bf16[8,40,128]{2,1,0:T(8,128)(2,1)S(1)} %all_to_all.10.own_ref), channel_id=1, source_target_pairs={{0,496},{16,32},{32,16},{48,64},{64,48},{80,96},{96,80},{112,128},... | collective-permute-start | bytes 245768 | tf_op jit(solution)/shard_map/ppermute | solution.py:161
